TPU v7x, 32 devices: a whole 2x2x4 slice. The times are simulated.
32 devices in a mesh: dp: 2 (over x), expert: 4 (over z), seq: 4 (over y, core).
Axes of the slice: x: 2, y: 2, z: 4, core: 2. Of those that a mesh axis runs over, the one named last changes fastest.
Arguments:
- tokens: bfloat16 [4096, 1024], P(('dp', 'expert', 'seq')), parts along dimension 0, may hold values from -6 to 6
- picks: int32 [32, 4, 16], P(('dp', 'expert', 'seq')), parts along dimension 0, may hold values from 0 to 127, as said below
- gates: float32 [32, 4, 16], P(('dp', 'expert', 'seq')), parts along dimension 0, may hold values from 0.1 to 2
- counts: int32 [32, 4], P(('dp', 'expert', 'seq')), parts along dimension 0, may hold values from 1 to 16, as said below
- norm_in: float32 [1024], replicated, may hold values from 0.1 to 1.9
- norm_out: float32 [1024], replicated, may hold values from 0.1 to 1.9
- w_in: bfloat16 [4, 1024, 1408], P('expert'), may hold values from -0.1875 to 0.1875
- w_out: bfloat16 [4, 1408, 1024], P('expert'), may hold values from -0.15625 to 0.15625
- w_key: bfloat16 [1024, 512], replicated, may hold values from -0.1875 to 0.1875
- w_value: bfloat16 [1024, 512], replicated, may hold values from -0.1875 to 0.1875
- queries: bfloat16 [1024, 512], P(('dp', 'expert', 'seq')), parts along dimension 0, may hold values from -300 to 300
- w_proj: bfloat16 [512, 1024], replicated, may hold values from -0.25 to 0.25
Outputs:
- encoded: bfloat16 [4096, 1024], P(('dp', 'expert', 'seq')), parts along dimension 0
- dec_out: bfloat16 [1024, 1024], P(('dp', 'expert', 'seq')), parts along dimension 0
There are 2 independent parts, one for each index of `dp`. A program takes and returns all parts, laid end to end along the dimension named above; an argument that names none is the same for every part. Nothing has to cross between parts.
Inputs may be any that keep to these rules, and one draw needn't show every extreme that they name: `picks`: for each source device and expert, 16 different row numbers of that device's 128 tokens. Slots c < counts are live, the rest are padding; some source device and expert has all 16 slots live.
All inputs are finite; a program needn't handle non-finite values.
Results may differ from a plain program's by a relative error of at most 0.015.
The roundings to bfloat16 on the way count: a program that leaves them out, or rounds other values in their place, can miss the bound.
Values may be sent and summed in bfloat16 or wider, within the bound.
A program may use at most 64 MiB of HBM per device.

v0:
```python
import jax
import jax.numpy as jnp
from jax import lax
from jax.sharding import PartitionSpec as P

HEADS = 8


EPSILON = 1e-06


def rms_norm(values, gain):
    mean_square = jnp.mean(values * values, axis=-1, keepdims=True)
    return values * lax.rsqrt(mean_square + EPSILON) * gain


def absorb(running, pieces, query_heads, score_scale):
    row_max, row_total, weighted = running
    key_piece, value_piece = pieces
    head_size = query_heads.shape[2]
    key_heads = key_piece.reshape(key_piece.shape[0], HEADS, head_size)
    value_heads = value_piece.reshape(value_piece.shape[0], HEADS, head_size)
    scores = (
        jnp.einsum("qhd,khd->qhk", query_heads, key_heads, preferred_element_type=jnp.float32)
        * score_scale
    )
    new_max = jnp.maximum(row_max, jnp.max(scores, axis=-1))
    weights = jnp.exp(scores - new_max[..., None])
    row_total = jnp.sum(weights, axis=-1)
    weighted = jnp.einsum(
        "qhk,khd->qhd",
        weights.astype(jnp.bfloat16),
        value_heads,
        preferred_element_type=jnp.float32,
    )
    return (new_max, row_total, weighted)


def starting(rows_count, head_size):
    return (
        jnp.full((rows_count, HEADS), -1e30, jnp.float32),
        jnp.zeros((rows_count, HEADS), jnp.float32),
        jnp.zeros((rows_count, HEADS, head_size), jnp.float32),
    )


def local(
    tokens, picks, gates, counts, norm_in, norm_out, w_in, w_out, w_key, w_value, queries, w_proj
):
    tok_rows, model_width = tokens.shape
    expert_total, slot_total = (picks.shape[1], picks.shape[2])
    plain = tokens.astype(jnp.float32)
    normed = rms_norm(plain, norm_in).astype(jnp.bfloat16)
    slot_index = picks[0].reshape(-1)
    outgoing = jnp.take(normed, slot_index, axis=0).reshape(expert_total, slot_total, model_width)
    slot_rows = lax.all_to_all(outgoing, "expert", split_axis=0, concat_axis=0, tiled=True)
    sources = slot_rows.shape[0]
    items = slot_rows.shape[1]
    flat = slot_rows.reshape(sources * items, model_width)
    hidden = jax.nn.gelu(
        jnp.dot(flat, w_in[0], preferred_element_type=jnp.float32), approximate=True
    ).astype(jnp.bfloat16)
    result = jnp.dot(hidden, w_out[0], preferred_element_type=jnp.float32).astype(jnp.bfloat16)
    returned = lax.all_to_all(
        result.reshape(sources, items, model_width),
        "expert",
        split_axis=0,
        concat_axis=0,
        tiled=True,
    )
    live_slots = lax.broadcasted_iota(jnp.int32, (expert_total, slot_total), 1) < counts[0][:, None]
    slot_weight = (gates[0] * live_slots.astype(jnp.float32)).reshape(-1)
    positions = lax.broadcasted_iota(jnp.int32, (tok_rows, expert_total * slot_total), 0)
    onehot = jnp.where(positions == slot_index[None, :], slot_weight[None, :], 0.0)
    expert_sum = jnp.dot(
        onehot,
        returned.reshape(-1, model_width).astype(jnp.float32),
        precision=lax.Precision.HIGHEST,
    )
    mixed = plain + expert_sum
    encoded = rms_norm(mixed, norm_out).astype(jnp.bfloat16)
    key_proj = jnp.dot(encoded, w_key, preferred_element_type=jnp.float32).astype(jnp.bfloat16)
    value_proj = jnp.dot(encoded, w_value, preferred_element_type=jnp.float32).astype(jnp.bfloat16)
    dec_rows = queries.shape[0]
    head_size = queries.shape[1] // HEADS
    score_scale = head_size ** (-0.5)
    query_heads = queries.reshape(dec_rows, HEADS, head_size)
    row_max, row_total, weighted = absorb(
        starting(dec_rows, head_size),
        (
            lax.all_gather(key_proj, "seq", axis=0, tiled=True),
            lax.all_gather(value_proj, "seq", axis=0, tiled=True),
        ),
        query_heads,
        score_scale,
    )
    context = (
        (weighted / row_total[..., None]).reshape(dec_rows, HEADS * head_size).astype(jnp.bfloat16)
    )
    dec_out = jnp.dot(context, w_proj, preferred_element_type=jnp.float32).astype(jnp.bfloat16)
    return (encoded, dec_out)


def solution(mesh):
    in_specs = (
        P(("dp", "expert", "seq"), None),
        P(("dp", "expert", "seq"), None, None),
        P(("dp", "expert", "seq"), None, None),
        P(("dp", "expert", "seq"), None),
        P(),
        P(),
        P("expert", None, None),
        P("expert", None, None),
        P(),
        P(),
        P(("dp", "expert", "seq"), None),
        P(),
    )
    out_specs = (P(("dp", "expert", "seq"), None), P(("dp", "expert", "seq"), None))
    return jax.shard_map(local, mesh=mesh, in_specs=in_specs, out_specs=out_specs, check_vma=False)
```

profile of v0, /device:TPU:0, one launch (start us, length us, event | category | flops | bytes accessed | tf_op | source)
XLA Modules:
  0.0 61.7 jit_solution(13997337401672658252)
XLA Ops:
  0.6 0.0 copy-start
  0.6 0.9 %reshape_squeeze.3 = s32[64,1]{0,1:T(1,128)S(1)} reshape(s32[1,4,16]{2,1,0:T(4,128)} %param.13) | data formatting | bytes 512 | tf_op jit(solution)/shard_map/reshape;squeeze | solution.py:54
  1.6 0.7 %compare_and_fusion = pred[4,16]{1,0:T(4,128)(4,1)S(1)} fusion(s32[1,4,16]{2,1,0:T(4,128)} %param.13), kind=kLoop, calls=%fused_computation.51 | loop fusion | flops 384 | bytes 320 | tf_op jit(solution)/shard_map/jit(_take)/and | solution.py:55
  2.2 1.1 %fusion.10 = f32[128]{0:T(128)S(1)} fusion(bf16[128,1024]{1,0:T(8,128)(2,1)} %param.12), kind=kLoop, calls=%fused_computation.18 | loop fusion | flops 393088 | bytes 262656 | tf_op jit(solution)/shard_map/reduce_sum | solution.py:13
  3.4 1.1 %fusion.12 = bf16[128,1024]{1,0:T(8,128)(2,1)S(1)} fusion(bf16[128,1024]{1,0:T(8,128)(2,1)} %param.12, f32[1024]{0:T(1024)} %param.16, f32[128]{0:T(128)S(1)} %add_rsqrt_fusion.1), kind=kLoop, calls=%fused_computation.20 | loop fusion | flops 524288 | bytes 528896 | tf_op jit(solution)/shard_map/convert_element_type | solution.py:53
  4.5 0.7 %gather_fusion = bf16[64,1024]{1,0:T(8,128)(2,1)S(1)} fusion(bf16[128,1024]{1,0:T(8,128)(2,1)S(1)} %fusion.12, s32[1024]{0:T(1024)S(1)} %pad_clamp_fusion), kind=kCustom, calls=%fused_computation | custom fusion | bytes 262400 | tf_op jit(solution)/shard_map/jit(_take)/gather | solution.py:55
  5.2 0.7 %broadcast_select_fusion = bf16[4,16,1024]{2,1,0:T(8,128)(2,1)} fusion(bf16[4,16,1024]{2,1,0:T(8,128)(2,1)S(1)} %bitcast.47, pred[4,16]{1,0:T(4,128)(4,1)S(1)} %compare_and_fusion), kind=kLoop, calls=%fused_computation.39 | loop fusion | flops 65536 | bytes 262208 | tf_op jit(solution)/shard_map/jit(_take)/select_n | solution.py:55
  5.9 6.3 %all-to-all-start = ((bf16[4,16,1024]{2,1,0:T(8,128)(2,1)}), bf16[4,16,1024]{2,1,0:T(8,128)(2,1)S(1)}, u32[]{:S(2)}, u32[]{:S(2)}) async-start(bf16[4,16,1024]{2,1,0:T(8,128)(2,1)} %broadcast_select_fusion), calls=%async_computation | async-start | bytes 262144 | tf_op jit(solution)/shard_map/all_to_all | solution.py:56
  12.2 0.8 %eq.12 = s32[64]{0:T(128)S(1)} reshape(s32[1,4,16]{2,1,0:T(4,128)} %param.13) | data formatting | bytes 512 | tf_op jit(solution)/shard_map/eq | solution.py:74
  13.0 0.7 %iota_compare_fusion.2 = pred[4,16]{1,0:T(4,128)(4,1)S(1)} fusion(s32[4]{0:T(128)} %bitcast.50), kind=kLoop, calls=%fused_computation.50 | loop fusion | flops 64 | bytes 80 | tf_op jit(solution)/shard_map/lt | solution.py:71
  13.7 0.1 lt.42
  13.8 0.8 %squeeze.9 = f32[64]{0:T(128)S(1)} reshape(f32[1,4,16]{2,1,0:T(4,128)} %param.14) | data formatting | bytes 512 | tf_op jit(solution)/shard_map/squeeze | solution.py:72
  14.6 0.9 %reshape.113 = bf16[32,8,64]{2,1,0:T(8,128)(2,1)S(1)} reshape(bf16[32,512]{1,0:T(8,128)(2,1)} %param.22) | data formatting | bytes 65536 | tf_op jit(solution)/shard_map/reshape | solution.py:87
  15.5 2.9 %all-to-all-done = bf16[4,16,1024]{2,1,0:T(8,128)(2,1)S(1)} async-done(((bf16[4,16,1024]{2,1,0:T(8,128)(2,1)}), bf16[4,16,1024]{2,1,0:T(8,128)(2,1)S(1)}, u32[]{:S(2)}, u32[]{:S(2)}) %all-to-all-start) | async-done | bytes 131104 | tf_op jit(solution)/shard_map/all_to_all | solution.py:56
  18.3 0.0 copy-done
  18.3 0.0 copy-start.1
  18.3 0.0 copy-start.3
  18.3 3.6 %fusion.5 = bf16[64,1024]{1,0:T(8,128)(2,1)} fusion(bf16[1,1408,1024]{2,1,0:T(8,128)(2,1)S(1)} %copy-done, bf16[64,1024]{1,0:T(8,128)(2,1)S(1)} %bitcast.46, bf16[1,1024,1408]{2,1,0:T(8,128)(2,1)} %param.18), kind=kOutput, calls=%fused_computation.8 | convolution fusion | flops 369975296 | bytes 6029312 | tf_op jit(solution)/shard_map/dot_general | solution.py:63
  22.0 3.3 %all-to-all-start.1 = ((bf16[4,16,1024]{2,1,0:T(8,128)(2,1)}), bf16[4,16,1024]{2,1,0:T(8,128)(2,1)S(1)}, u32[]{:S(2)}, u32[]{:S(2)}) async-start(bf16[4,16,1024]{2,1,0:T(8,128)(2,1)} %bitcast.7), calls=%async_computation.1 | async-start | bytes 262144 | tf_op jit(solution)/shard_map/all_to_all | solution.py:64
  25.3 5.9 %all-to-all-done.1 = bf16[4,16,1024]{2,1,0:T(8,128)(2,1)S(1)} async-done(((bf16[4,16,1024]{2,1,0:T(8,128)(2,1)}), bf16[4,16,1024]{2,1,0:T(8,128)(2,1)S(1)}, u32[]{:S(2)}, u32[]{:S(2)}) %all-to-all-start.1) | async-done | bytes 131104 | tf_op jit(solution)/shard_map/all_to_all | solution.py:64
  31.2 0.0 copy-done.1
  31.2 0.5 multiply_reduce_fusion
  31.7 0.0 copy-done.3
  31.7 0.1 multiply_convert_fusion
  31.8 0.0 copy-start.2
  31.8 1.6 %convolution_convert_fusion = bf16[128,512]{1,0:T(8,128)(2,1)S(1)} fusion(bf16[128,1024]{1,0:T(8,128)(2,1)S(1)} %multiply_convert_fusion, bf16[1024,512]{1,0:T(8,128)(2,1)} %param.20), kind=kOutput, calls=%fused_computation.9 | convolution fusion | flops 134283264 | bytes 1441792 | tf_op jit(solution)/shard_map/dot_general | solution.py:82
  33.5 7.7 %all_gather.7 = bf16[512,512]{1,0:T(8,128)(2,1)} all-gather(bf16[128,512]{1,0:T(8,128)(2,1)S(1)} %convolution_convert_fusion), channel_id=1, replica_groups=mesh['dp'=2,'expert'=4,'seq'=4] {'seq'}, dimensions={0}, use_global_device_ids=true | all-gather | bytes 655360 | tf_op jit(solution)/shard_map/all_gather | solution.py:91
  41.1 2.1 %copy.18 = bf16[512,512]{0,1:T(8,128)(2,1)} copy(bf16[512,512]{1,0:T(8,128)(2,1)} %all_gather.7) | data formatting | bytes 1048576 | tf_op jit(solution)/shard_map/all_gather | solution.py:91
  43.2 2.0 %fusion.46 = (f32[32,8]{0,1:T(8,128)S(1)}, f32[32,8,512]{2,0,1:T(8,128)}) fusion(bf16[512,8,64]{0,2,1:T(8,128)(2,1)} %bitcast.45, bf16[32,8,64]{2,1,0:T(8,128)(2,1)S(1)} %reshape.113), kind=kOutput, calls=%fused_computation.61 | convolution fusion | flops 17039104 | bytes 1082368 | tf_op jit(solution)/shard_map/qhd,khd->qhk/dot_general | solution.py:24
  45.2 1.5 %convolution_convert_fusion.1 = bf16[128,512]{1,0:T(8,128)(2,1)S(1)} fusion(bf16[128,1024]{1,0:T(8,128)(2,1)S(1)} %multiply_convert_fusion, bf16[1024,512]{1,0:T(8,128)(2,1)} %param.21), kind=kOutput, calls=%fused_computation.10 | convolution fusion | flops 134283264 | bytes 1441792 | tf_op jit(solution)/shard_map/dot_general | solution.py:83
  46.8 7.7 %all_gather.6 = bf16[512,512]{1,0:T(8,128)(2,1)} all-gather(bf16[128,512]{1,0:T(8,128)(2,1)S(1)} %convolution_convert_fusion.1), channel_id=1, replica_groups=mesh['dp'=2,'expert'=4,'seq'=4] {'seq'}, dimensions={0}, use_global_device_ids=true | all-gather | bytes 655360 | tf_op jit(solution)/shard_map/all_gather | solution.py:92
  54.5 0.0 copy-done.2
  54.5 2.1 %copy.17 = bf16[512,512]{0,1:T(8,128)(2,1)} copy(bf16[512,512]{1,0:T(8,128)(2,1)} %all_gather.6) | data formatting | bytes 1048576 | tf_op jit(solution)/shard_map/all_gather | solution.py:92
  56.6 1.3 %fusion.13 = f32[32,8]{0,1:T(8,128)S(1)} fusion(f32[32,8,512]{2,0,1:T(8,128)} %get-tuple-element.5, f32[32,8]{0,1:T(8,128)S(1)} %broadcast_maximum_fusion), kind=kLoop, calls=%fused_computation.24 | loop fusion | flops 261888 | bytes 526336 | tf_op jit(solution)/shard_map/reduce_sum | solution.py:29
  57.8 1.5 %fusion.9 = bf16[32,8,64]{2,0,1:T(8,128)(2,1)S(1)} fusion(bf16[512,8,64]{0,2,1:T(8,128)(2,1)} %bitcast.48, f32[32,8,512]{2,0,1:T(8,128)} %get-tuple-element.5, f32[32,8]{0,1:T(8,128)S(1)} %broadcast_maximum_fusion, f32[32,8]{0,1:T(8,128)S(1)} %fusion.13), kind=kOutput, calls=%fused_computation.13 | convolution fusion | flops 17072128 | bytes 1083392 | tf_op jit(solution)/shard_map/qhk,khd->qhd/dot_general | solution.py:30
  59.4 0.1 convert_element_type.44
  59.5 2.1 %convolution_convert_fusion.2 = bf16[32,1024]{1,0:T(8,128)(2,1)} fusion(bf16[32,512]{1,0:T(8,128)(2,1)S(1)} %convert_element_type.44, bf16[512,1024]{1,0:T(8,128)(2,1)} %param.23), kind=kOutput, calls=%fused_computation.14 | convolution fusion | flops 33587200 | bytes 1146880 | tf_op jit(solution)/shard_map/dot_general | solution.py:100
  (7 shorter events, 0.1 us)
Async XLA Ops:
  0.6 17.7 %copy-start = (bf16[1,1408,1024]{2,1,0:T(8,128)(2,1)S(1)}, bf16[1,1408,1024]{2,1,0:T(8,128)(2,1)}, u32[]{:S(2)}) copy-start(bf16[1,1408,1024]{2,1,0:T(8,128)(2,1)} %param.19) | copy-start | bytes 8650756
  5.9 12.4 %all-to-all-start = ((bf16[4,16,1024]{2,1,0:T(8,128)(2,1)}), bf16[4,16,1024]{2,1,0:T(8,128)(2,1)S(1)}, u32[]{:S(2)}, u32[]{:S(2)}) async-start(bf16[4,16,1024]{2,1,0:T(8,128)(2,1)} %broadcast_select_fusion), calls=%async_computation | async-start | bytes 262144 | tf_op jit(solution)/shard_map/all_to_all | solution.py:56
  18.3 12.9 %copy-start.1 = (bf16[128,1024]{1,0:T(8,128)(2,1)S(1)}, bf16[128,1024]{1,0:T(8,128)(2,1)}, u32[]{:S(2)}) copy-start(bf16[128,1024]{1,0:T(8,128)(2,1)} %param.12) | copy-start | bytes 786436
  18.3 13.4 %copy-start.3 = (f32[1024]{0:T(1024)S(1)}, f32[1024]{0:T(1024)}, u32[]{:S(2)}) copy-start(f32[1024]{0:T(1024)} %param.17) | copy-start | bytes 12292
  22.0 9.2 %all-to-all-start.1 = ((bf16[4,16,1024]{2,1,0:T(8,128)(2,1)}), bf16[4,16,1024]{2,1,0:T(8,128)(2,1)S(1)}, u32[]{:S(2)}, u32[]{:S(2)}) async-start(bf16[4,16,1024]{2,1,0:T(8,128)(2,1)} %bitcast.7), calls=%async_computation.1 | async-start | bytes 262144 | tf_op jit(solution)/shard_map/all_to_all | solution.py:64
  31.8 22.7 %copy-start.2 = (bf16[128,1024]{1,0:T(8,128)(2,1)}, bf16[128,1024]{1,0:T(8,128)(2,1)S(1)}, u32[]{:S(2)}) copy-start(bf16[128,1024]{1,0:T(8,128)(2,1)S(1)} %multiply_convert_fusion) | copy-start | bytes 786436
where the time goes:
time: 62.5 us; the launch traced here: 61.7 us
  blocking collectives  15.4 us (25%)
  matrix products  13 us (21%)
  starting transfers between devices  9.67 us (15%)
  waiting for transfers between devices  8.74 us (14%)
  local copies, waits for them, and re-layouts  8.4 us (13%)
  other arithmetic  5.73 us (9%)
  between operations  0.75 us (1%)
    all_gather x1, blocking collectives, local(): lax.all_gather(value_proj, 'seq', axis=0, tiled=True)  7.73 us
    all_gather x1, blocking collectives, local(): lax.all_gather(key_proj, 'seq', axis=0, tiled=True)  7.65 us
    all_to_all x1, starting transfers between devices, local(): lax.all_to_all(outgoing, 'expert', split_axis=0, concat_axis=0, tiled=True)  6.35 us
    all_to_all x1, waiting for transfers between devices, local(): lax.all_to_all(result.reshape(sources, items, model_width), 'expert', spl...  5.87 us
    dot_general x1, matrix products, local(): jnp.dot(hidden, w_out[0], preferred_element_type=jnp.float32)  3.65 us
    all_to_all x1, starting transfers between devices, local(): lax.all_to_all(result.reshape(sources, items, model_width), 'expert', spl...  3.33 us
    all_to_all x1, waiting for transfers between devices, local(): lax.all_to_all(outgoing, 'expert', split_axis=0, concat_axis=0, tiled=True)  2.86 us
    dot_general x1, matrix products, local(): jnp.dot(context, w_proj, preferred_element_type=jnp.float32)  2.15 us
  transfers between devices with their start and end apart: 2, of which 2 were waited for; matrix products, arithmetic and copies ran while one was open for 5% of the time, Pallas kernels for 0%

commit v1 on v0

v1 whole, which is shorter than its diff:
```python
import functools

import jax
import jax.numpy as jnp
from jax import lax
from jax.experimental import pallas as pl
from jax.experimental.pallas import tpu as pltpu
from jax.sharding import PartitionSpec as P

HEADS = 8
EPSILON = 1e-06
MESH = pl.DeviceIdType.MESH
F32 = jnp.float32
BF16 = jnp.bfloat16


def rms_norm(values, gain):
    mean_square = jnp.mean(values * values, axis=-1, keepdims=True)
    return values * lax.rsqrt(mean_square + EPSILON) * gain


def gelu(v):
    return 0.5 * v * (1.0 + jnp.tanh(0.7978845608028654 * (v + 0.044715 * v * v * v)))


def kernel(
    n_e,
    n_s,
    tokens_h,
    picks_h,
    gates_h,
    counts_h,
    norm_in_h,
    norm_out_h,
    w_in_h,
    w_out_h,
    w_key_h,
    w_value_h,
    queries_h,
    w_proj_h,
    encoded_h,
    dec_h,
    tokens_v,
    picks_v,
    gates_v,
    counts_v,
    norm_in_v,
    norm_out_v,
    w_in_v,
    w_out_v,
    w_key_v,
    w_value_v,
    q_v,
    w_proj_v,
    send_a,
    recv_a,
    send_b,
    recv_b,
    enc_v,
    part_v,
    stat_v,
    part_r,
    stat_r,
    dec_v,
    load_sem,
    store_sem,
    a_send,
    a_recv,
    b_send,
    b_recv,
    q_send,
    q_recv,
    p_send,
    p_recv,
    s_send,
    s_recv,
):
    me_e = lax.axis_index("expert")
    me_s = lax.axis_index("seq")
    rows, width = tokens_v.shape
    slots = send_a.shape[1]
    dec_rows = q_v.shape[1]
    q_width = q_v.shape[2]
    head = q_width // HEADS

    loads = {}
    for i, (name, src, dst) in enumerate(
        (
            ("tokens", tokens_h, tokens_v),
            ("norm_in", norm_in_h, norm_in_v),
            ("picks", picks_h, picks_v),
            ("queries", queries_h, q_v.at[me_s]),
            ("w_in", w_in_h.at[0], w_in_v),
            ("w_out", w_out_h.at[0], w_out_v),
            ("gates", gates_h, gates_v),
            ("counts", counts_h, counts_v),
            ("norm_out", norm_out_h, norm_out_v),
            ("w_key", w_key_h, w_key_v),
            ("w_value", w_value_h, w_value_v),
            ("w_proj", w_proj_h, w_proj_v),
        )
    ):
        loads[name] = pltpu.make_async_copy(src, dst, load_sem.at[i])
        loads[name].start()

    barrier = pltpu.get_barrier_semaphore()
    for d in range(1, n_e):
        pl.semaphore_signal(
            barrier, inc=1, device_id={"expert": lax.rem(me_e + d, n_e)}, device_id_type=MESH
        )
    for d in range(1, n_s):
        pl.semaphore_signal(
            barrier, inc=1, device_id={"seq": lax.rem(me_s + d, n_s)}, device_id_type=MESH
        )

    loads["tokens"].wait()
    loads["norm_in"].wait()
    loads["picks"].wait()
    normed = rms_norm(tokens_v[...].astype(F32), norm_in_v[...]).astype(BF16)
    pick_row = jnp.concatenate([picks_v[0, j : j + 1, :] for j in range(n_e)], axis=1)
    position = lax.broadcasted_iota(jnp.int32, (rows, n_e * slots), 0)
    chosen = jnp.where(position == pick_row, 1.0, 0.0).astype(BF16)
    outgoing = lax.dot_general(
        chosen, normed, (((0,), (0,)), ((), ())), preferred_element_type=F32
    ).astype(BF16)
    send_a[...] = outgoing.reshape(n_e, slots, width)
    pl.semaphore_wait(barrier, n_e - 1 + n_s - 1)

    a_copies = []
    for d in range(1, n_e):
        to = lax.rem(me_e + d, n_e)
        copy = pltpu.make_async_remote_copy(
            src_ref=send_a.at[to],
            dst_ref=recv_a.at[d],
            send_sem=a_send.at[d],
            recv_sem=a_recv.at[d],
            device_id={"expert": to},
            device_id_type=MESH,
        )
        copy.start()
        a_copies.append(copy)
    loads["queries"].wait()
    q_copies = []
    for d in range(1, n_s):
        copy = pltpu.make_async_remote_copy(
            src_ref=q_v.at[me_s],
            dst_ref=q_v.at[me_s],
            send_sem=q_send.at[d],
            recv_sem=q_recv.at[d],
            device_id={"seq": lax.rem(me_s + d, n_s)},
            device_id_type=MESH,
        )
        copy.start()
        q_copies.append(copy)
    recv_a[0] = send_a[me_e]

    loads["gates"].wait()
    loads["counts"].wait()
    slot = lax.broadcasted_iota(jnp.int32, (1, slots), 1)
    gate_row = jnp.concatenate(
        [
            jnp.where(slot < counts_v[0:1, j : j + 1], gates_v[0, j : j + 1, :], 0.0)
            for j in range(n_e)
        ],
        axis=1,
    )
    high = gate_row.astype(BF16).astype(F32)
    middle = (gate_row - high).astype(BF16).astype(F32)
    low = gate_row - high - middle
    gate_three = jnp.concatenate([high, middle, low], axis=1)
    pick_three = jnp.concatenate([pick_row] * 3, axis=1)
    position_three = lax.broadcasted_iota(jnp.int32, (rows, 3 * n_e * slots), 0)
    combine = jnp.where(position_three == pick_three, gate_three, 0.0).astype(BF16)

    loads["w_in"].wait()
    for copy in a_copies:
        copy.wait_recv()
    flat = recv_a[...].reshape(n_e * slots, width)
    hidden = gelu(jnp.dot(flat, w_in_v[...], preferred_element_type=F32)).astype(BF16)
    loads["w_out"].wait()
    result = jnp.dot(hidden, w_out_v[...], preferred_element_type=F32).astype(BF16)
    send_b[...] = result.reshape(n_e, slots, width)
    b_copies = []
    for d in range(1, n_e):
        copy = pltpu.make_async_remote_copy(
            src_ref=send_b.at[d],
            dst_ref=recv_b.at[me_e],
            send_sem=b_send.at[d],
            recv_sem=b_recv.at[d],
            device_id={"expert": lax.rem(me_e + n_e - d, n_e)},
            device_id_type=MESH,
        )
        copy.start()
        b_copies.append(copy)
    recv_b[me_e] = send_b[0]

    loads["norm_out"].wait()
    loads["w_key"].wait()
    loads["w_value"].wait()
    for d in range(1, n_e):
        pltpu.make_async_remote_copy(
            src_ref=send_b.at[d],
            dst_ref=recv_b.at[lax.rem(me_e + d, n_e)],
            send_sem=b_send.at[d],
            recv_sem=b_recv.at[d],
            device_id={"expert": lax.rem(me_e + n_e - d, n_e)},
            device_id_type=MESH,
        ).wait_recv()
    returned = recv_b[...].reshape(n_e * slots, width)
    expert_sum = jnp.dot(
        combine, jnp.concatenate([returned] * 3, axis=0), preferred_element_type=F32
    )
    mixed = tokens_v[...].astype(F32) + expert_sum
    encoded = rms_norm(mixed, norm_out_v[...]).astype(BF16)
    enc_v[...] = encoded
    enc_store = pltpu.make_async_copy(enc_v, encoded_h, store_sem.at[0])
    enc_store.start()
    keys = jnp.dot(encoded, w_key_v[...], preferred_element_type=F32).astype(BF16)
    values = jnp.dot(encoded, w_value_v[...], preferred_element_type=F32).astype(BF16)

    for d in range(1, n_s):
        pltpu.make_async_remote_copy(
            src_ref=q_v.at[me_s],
            dst_ref=q_v.at[lax.rem(me_s + n_s - d, n_s)],
            send_sem=q_send.at[d],
            recv_sem=q_recv.at[d],
            device_id={"seq": lax.rem(me_s + d, n_s)},
            device_id_type=MESH,
        ).wait_recv()
    all_rows = n_s * dec_rows
    queries = q_v[...].reshape(all_rows, q_width)
    slab = min(256, q_width)
    group = slab // head
    lane_head = lax.broadcasted_iota(jnp.int32, (1, slab), 1) // head
    stat_lane = lax.broadcasted_iota(jnp.int32, (1, stat_v.shape[2]), 1)
    stats = jnp.zeros((all_rows, stat_v.shape[2]), F32)
    for g in range(q_width // slab):
        cols = slice(g * slab, (g + 1) * slab)
        stacked = jnp.concatenate(
            [
                queries[:, cols] * jnp.where(lane_head == h, 1.0, 0.0).astype(BF16)
                for h in range(group)
            ],
            axis=0,
        )
        scores = lax.dot_general(
            stacked, keys[:, cols], (((1,), (1,)), ((), ())), preferred_element_type=F32
        ) * (head**-0.5)
        row_max = jnp.max(scores, axis=1, keepdims=True)
        weights = jnp.exp(scores - row_max)
        row_total = jnp.sum(weights, axis=1, keepdims=True)
        product = jnp.dot(weights.astype(BF16), values[:, cols], preferred_element_type=F32)
        joined = product[:all_rows]
        for h in range(group):
            span = slice(h * all_rows, (h + 1) * all_rows)
            if h:
                joined = jnp.where(lane_head == h, product[span], joined)
            at = g * group + h
            stats = jnp.where(stat_lane == at, row_max[span], stats)
            stats = jnp.where(stat_lane == HEADS + at, row_total[span], stats)
        part_v[:, :, cols] = joined.astype(BF16).reshape(n_s, dec_rows, slab)
    stat_v[...] = stats.reshape(n_s, dec_rows, stat_v.shape[2])

    p_copies = []
    for d in range(1, n_s):
        to = lax.rem(me_s + d, n_s)
        for src, dst, ss, rs in (
            (stat_v, stat_r, s_send, s_recv),
            (part_v, part_r, p_send, p_recv),
        ):
            copy = pltpu.make_async_remote_copy(
                src_ref=src.at[to],
                dst_ref=dst.at[d],
                send_sem=ss.at[d],
                recv_sem=rs.at[d],
                device_id={"seq": to},
                device_id_type=MESH,
            )
            copy.start()
            p_copies.append(copy)
    loads["w_proj"].wait()
    for copy in p_copies:
        copy.wait_recv()
    part = [part_v[me_s].astype(F32)] + [part_r[d].astype(F32) for d in range(1, n_s)]
    stat = [stat_v[me_s]] + [stat_r[d] for d in range(1, n_s)]
    top = functools.reduce(jnp.maximum, stat)
    factor = [jnp.exp(s - top)[:, :HEADS] for s in stat]
    total = sum(f * s[:, HEADS : 2 * HEADS] for f, s in zip(factor, stat))
    lane = lax.broadcasted_iota(jnp.int32, (1, q_width), 1) // head
    summed = jnp.zeros((dec_rows, q_width), F32)
    for f, p in zip(factor, part):
        scale = f / total
        spread = jnp.zeros((dec_rows, q_width), F32)
        for h in range(HEADS):
            spread = jnp.where(lane == h, scale[:, h : h + 1], spread)
        summed = summed + spread * p
    dec_v[...] = jnp.dot(
        summed.astype(BF16), w_proj_v[...], preferred_element_type=F32
    ).astype(BF16)
    dec_store = pltpu.make_async_copy(dec_v, dec_h, store_sem.at[1])
    dec_store.start()
    for copy in a_copies + b_copies + q_copies + p_copies:
        copy.wait_send()
    enc_store.wait()
    dec_store.wait()


def local(
    n_e,
    n_s,
    tokens,
    picks,
    gates,
    counts,
    norm_in,
    norm_out,
    w_in,
    w_out,
    w_key,
    w_value,
    queries,
    w_proj,
):
    rows, width = tokens.shape
    slots = picks.shape[2]
    hidden = w_in.shape[2]
    dec_rows, q_width = queries.shape
    lanes = max(128, 2 * HEADS)
    anywhere = pl.BlockSpec(memory_space=pl.ANY)
    dma = pltpu.SemaphoreType.DMA
    return pl.pallas_call(
        functools.partial(kernel, n_e, n_s),
        out_shape=(
            jax.ShapeDtypeStruct((rows, width), BF16),
            jax.ShapeDtypeStruct((dec_rows, width), BF16),
        ),
        in_specs=[anywhere] * 12,
        out_specs=(anywhere, anywhere),
        scratch_shapes=[
            pltpu.VMEM((rows, width), BF16),
            pltpu.VMEM(picks.shape, jnp.int32),
            pltpu.VMEM(gates.shape, F32),
            pltpu.VMEM(counts.shape, jnp.int32),
            pltpu.VMEM((1, width), F32),
            pltpu.VMEM((1, width), F32),
            pltpu.VMEM((width, hidden), BF16),
            pltpu.VMEM((hidden, width), BF16),
            pltpu.VMEM((width, q_width), BF16),
            pltpu.VMEM((width, q_width), BF16),
            pltpu.VMEM((n_s, dec_rows, q_width), BF16),
            pltpu.VMEM((q_width, width), BF16),
            pltpu.VMEM((n_e, slots, width), BF16),
            pltpu.VMEM((n_e, slots, width), BF16),
            pltpu.VMEM((n_e, slots, width), BF16),
            pltpu.VMEM((n_e, slots, width), BF16),
            pltpu.VMEM((rows, width), BF16),
            pltpu.VMEM((n_s, dec_rows, q_width), BF16),
            pltpu.VMEM((n_s, dec_rows, lanes), F32),
            pltpu.VMEM((n_s, dec_rows, q_width), BF16),
            pltpu.VMEM((n_s, dec_rows, lanes), F32),
            pltpu.VMEM((dec_rows, width), BF16),
            dma((12,)),
            dma((2,)),
            dma((n_e,)),
            dma((n_e,)),
            dma((n_e,)),
            dma((n_e,)),
            dma((n_s,)),
            dma((n_s,)),
            dma((n_s,)),
            dma((n_s,)),
            dma((n_s,)),
            dma((n_s,)),
        ],
        compiler_params=pltpu.CompilerParams(collective_id=0, has_side_effects=True),
    )(
        tokens,
        picks,
        gates,
        counts,
        norm_in.reshape(1, -1),
        norm_out.reshape(1, -1),
        w_in,
        w_out,
        w_key,
        w_value,
        queries,
        w_proj,
    )


def solution(mesh):
    in_specs = (
        P(("dp", "expert", "seq"), None),
        P(("dp", "expert", "seq"), None, None),
        P(("dp", "expert", "seq"), None, None),
        P(("dp", "expert", "seq"), None),
        P(),
        P(),
        P("expert", None, None),
        P("expert", None, None),
        P(),
        P(),
        P(("dp", "expert", "seq"), None),
        P(),
    )
    out_specs = (P(("dp", "expert", "seq"), None), P(("dp", "expert", "seq"), None))
    body = functools.partial(local, mesh.shape["expert"], mesh.shape["seq"])
    return jax.shard_map(body, mesh=mesh, in_specs=in_specs, out_specs=out_specs, check_vma=False)
```

time: 62.5 us -> 26.2 us (0.42); the launches traced: 61.7 us -> 26 us
  Pallas kernels: 0 us -> 22.2 us
  blocking collectives: 15.4 us -> 0 us
  matrix products: 13 us -> 0 us
  starting transfers between devices: 9.67 us -> 0 us
  waiting for transfers between devices: 8.74 us -> 0 us
  other arithmetic: 5.73 us -> 0 us
  local copies, waits for them, and re-layouts: 8.4 us -> 3.14 us
    pallas_call x0 -> x1, Pallas kernels: none -> 22.2 us  [local(): pl.pallas_call(functools.partial(kernel, n_e, n_s), out_shape=(jax.ShapeD...]
    all_gather x2 -> x0, blocking collectives: 15.4 us -> none  [the longest x1 7.73 us: local(): lax.all_gather(value_proj, 'seq', axis=0, tiled=True)]
    dot_general x7 -> x0, matrix products: 13 us -> none  [the longest x1 3.65 us: local(): jnp.dot(hidden, w_out[0], preferred_element_type=jnp.float32)]
    all_to_all x2 -> x0, starting transfers between devices: 9.67 us -> none  [the longest x1 6.35 us: local(): lax.all_to_all(outgoing, 'expert', split_axis=0, concat_axis=0, tiled=True)]
    all_to_all x2 -> x0, waiting for transfers between devices: 8.74 us -> none  [the longest x1 5.87 us: local(): lax.all_to_all(result.reshape(sources, items, model_width), 'expert', spl...]
    all_gather x2 -> x0, local copies, waits for them, and re-layouts: 4.13 us -> none  [the longest x1 2.06 us: local(): lax.all_gather(value_proj, 'seq', axis=0, tiled=True)]
    unnamed x8 -> x2, local copies, waits for them, and re-layouts: 0.02 us -> 3.14 us
    reduce_sum x2 -> x0, other arithmetic: 2.34 us -> none  [the longest x1 1.26 us: absorb(): row_total = jnp.sum(weights, axis=-1)]
  transfers between devices with their start and end apart: 2 -> 0, of which waited for: 2 -> 0; matrix products, arithmetic and copies ran while one was open for 5% -> 0% of each run, Pallas kernels for 0% -> 0%
where the time goes in v1:
time: 26.2 us; the launch traced here: 26 us
  Pallas kernels  22.2 us (85%)
  local copies, waits for them, and re-layouts  3.14 us (12%)
  between operations  0.64 us (2%)
    pallas_call x1, Pallas kernels, local(): pl.pallas_call(functools.partial(kernel, n_e, n_s), out_shape=(jax.ShapeD...  22.2 us
    unnamed x2, local copies, waits for them, and re-layouts  3.14 us

profile of v1, /device:TPU:0, one launch (start us, length us, event | category | flops | bytes accessed | tf_op | source)
XLA Modules:
  0.0 26.0 jit_solution(196070315615506191)
XLA Ops:
  0.6 22.2 %shard_map.131 = (bf16[128,1024]{1,0:T(8,128)(2,1)}, bf16[32,1024]{1,0:T(8,128)(2,1)}) custom-call(bf16[128,1024]{1,0:T(8,128)(2,1)} %tokens_h.1, s32[1,4,16]{2,1,0:T(4,128)} %picks_h.1, f32[1,4,16]{2,1,0:T(4,128)} %gates_h.1, s32[1,4]{1,0:T(1,128)} %counts_h.1, f32[1,1024]{1,0:T(1,128)} %bitcast.2, f32[1,1024]{1,0:T(1,128)} %bitcast.3, ...), custom_call_target="tpu_custom_call" | custom-call | tf_op jit(solution)/shard_map/pallas_call | solution.py:331
  22.9 1.7 %copy.16 = bf16[128,1024]{1,0:T(8,128)(2,1)} copy(bf16[128,1024]{1,0:T(8,128)(2,1)} %get-tuple-element.4) | data formatting | bytes 524288
  24.5 1.5 %copy.17 = bf16[32,1024]{1,0:T(8,128)(2,1)} copy(bf16[32,1024]{1,0:T(8,128)(2,1)} %get-tuple-element.5) | data formatting | bytes 131072

commit v2 on v1

--- a/solution.py
+++ b/solution.py
@@ -9,6 +9,7 @@
 
 HEADS = 8
 EPSILON = 1e-06
+VMEM_BYTES = 67043328
 MESH = pl.DeviceIdType.MESH
 F32 = jnp.float32
 BF16 = jnp.bfloat16
@@ -38,8 +39,10 @@
     w_value_h,
     queries_h,
     w_proj_h,
-    encoded_h,
-    dec_h,
+    enc_v,
+    part_r,
+    stat_r,
+    w_proj_v,
     tokens_v,
     picks_v,
     gates_v,
@@ -51,19 +54,13 @@
     w_key_v,
     w_value_v,
     q_v,
-    w_proj_v,
     send_a,
     recv_a,
     send_b,
     recv_b,
-    enc_v,
     part_v,
     stat_v,
-    part_r,
-    stat_r,
-    dec_v,
     load_sem,
-    store_sem,
     a_send,
     a_recv,
     b_send,
@@ -213,8 +210,6 @@
     mixed = tokens_v[...].astype(F32) + expert_sum
     encoded = rms_norm(mixed, norm_out_v[...]).astype(BF16)
     enc_v[...] = encoded
-    enc_store = pltpu.make_async_copy(enc_v, encoded_h, store_sem.at[0])
-    enc_store.start()
     keys = jnp.dot(encoded, w_key_v[...], preferred_element_type=F32).astype(BF16)
     values = jnp.dot(encoded, w_value_v[...], preferred_element_type=F32).astype(BF16)
 
@@ -261,6 +256,8 @@
         part_v[:, :, cols] = joined.astype(BF16).reshape(n_s, dec_rows, slab)
     stat_v[...] = stats.reshape(n_s, dec_rows, stat_v.shape[2])
 
+    part_r[0] = part_v[me_s]
+    stat_r[0] = stat_v[me_s]
     p_copies = []
     for d in range(1, n_s):
         to = lax.rem(me_s + d, n_s)
@@ -278,11 +275,22 @@
             )
             copy.start()
             p_copies.append(copy)
-    loads["w_proj"].wait()
     for copy in p_copies:
         copy.wait_recv()
-    part = [part_v[me_s].astype(F32)] + [part_r[d].astype(F32) for d in range(1, n_s)]
-    stat = [stat_v[me_s]] + [stat_r[d] for d in range(1, n_s)]
+    for copy in a_copies + b_copies + q_copies + p_copies:
+        copy.wait_send()
+    loads["w_proj"].wait()
+
+
+def finish(
+    enc_v, part_v, stat_v, w_proj_v, encoded_h, dec_h, dec_v, store_sem
+):
+    enc_store = pltpu.make_async_copy(enc_v, encoded_h, store_sem.at[0])
+    enc_store.start()
+    n_s, dec_rows, q_width = part_v.shape
+    head = q_width // HEADS
+    part = [part_v[d].astype(F32) for d in range(n_s)]
+    stat = [stat_v[d] for d in range(n_s)]
     top = functools.reduce(jnp.maximum, stat)
     factor = [jnp.exp(s - top)[:, :HEADS] for s in stat]
     total = sum(f * s[:, HEADS : 2 * HEADS] for f, s in zip(factor, stat))
@@ -299,8 +307,6 @@
     ).astype(BF16)
     dec_store = pltpu.make_async_copy(dec_v, dec_h, store_sem.at[1])
     dec_store.start()
-    for copy in a_copies + b_copies + q_copies + p_copies:
-        copy.wait_send()
     enc_store.wait()
     dec_store.wait()
 
@@ -328,14 +334,18 @@
     lanes = max(128, 2 * HEADS)
     anywhere = pl.BlockSpec(memory_space=pl.ANY)
     dma = pltpu.SemaphoreType.DMA
-    return pl.pallas_call(
+    vmem = pl.BlockSpec(memory_space=pltpu.VMEM)
+    room = 2 * (rows * width + n_s * dec_rows * (q_width + 2 * lanes) + q_width * width)
+    encoded, part, stat, w_proj_near = pl.pallas_call(
         functools.partial(kernel, n_e, n_s),
         out_shape=(
-            jax.ShapeDtypeStruct((rows, width), BF16),
-            jax.ShapeDtypeStruct((dec_rows, width), BF16),
+            pltpu.VMEM((rows, width), BF16),
+            pltpu.VMEM((n_s, dec_rows, q_width), BF16),
+            pltpu.VMEM((n_s, dec_rows, lanes), F32),
+            pltpu.VMEM((q_width, width), BF16),
         ),
         in_specs=[anywhere] * 12,
-        out_specs=(anywhere, anywhere),
+        out_specs=(vmem, vmem, vmem, vmem),
         scratch_shapes=[
             pltpu.VMEM((rows, width), BF16),
             pltpu.VMEM(picks.shape, jnp.int32),
@@ -348,19 +358,13 @@
             pltpu.VMEM((width, q_width), BF16),
             pltpu.VMEM((width, q_width), BF16),
             pltpu.VMEM((n_s, dec_rows, q_width), BF16),
-            pltpu.VMEM((q_width, width), BF16),
             pltpu.VMEM((n_e, slots, width), BF16),
             pltpu.VMEM((n_e, slots, width), BF16),
             pltpu.VMEM((n_e, slots, width), BF16),
             pltpu.VMEM((n_e, slots, width), BF16),
-            pltpu.VMEM((rows, width), BF16),
             pltpu.VMEM((n_s, dec_rows, q_width), BF16),
             pltpu.VMEM((n_s, dec_rows, lanes), F32),
-            pltpu.VMEM((n_s, dec_rows, q_width), BF16),
-            pltpu.VMEM((n_s, dec_rows, lanes), F32),
-            pltpu.VMEM((dec_rows, width), BF16),
             dma((12,)),
-            dma((2,)),
             dma((n_e,)),
             dma((n_e,)),
             dma((n_e,)),
@@ -372,7 +376,9 @@
             dma((n_s,)),
             dma((n_s,)),
         ],
-        compiler_params=pltpu.CompilerParams(collective_id=0, has_side_effects=True),
+        compiler_params=pltpu.CompilerParams(
+            collective_id=0, has_side_effects=True, vmem_limit_bytes=VMEM_BYTES - room
+        ),
     )(
         tokens,
         picks,
@@ -387,6 +393,17 @@
         queries,
         w_proj,
     )
+    return pl.pallas_call(
+        finish,
+        out_shape=(
+            jax.ShapeDtypeStruct((rows, width), BF16),
+            jax.ShapeDtypeStruct((dec_rows, width), BF16),
+        ),
+        in_specs=[vmem] * 4,
+        out_specs=(anywhere, anywhere),
+        scratch_shapes=[pltpu.VMEM((dec_rows, width), BF16), dma((2,))],
+        compiler_params=pltpu.CompilerParams(vmem_limit_bytes=8 * 2**20),
+    )(encoded, part, stat, w_proj_near)
 
 
 def solution(mesh):

time: 26.2 us -> 23.1 us (0.88)
  local copies, waits for them, and re-layouts: 3.14 us -> 0 us
    unnamed x2 -> x0, local copies, waits for them, and re-layouts: 3.14 us -> none
    pallas_call x1 -> x2, Pallas kernels: 22.2 us -> 22.3 us  [the longest x1 21 us: local(): pl.pallas_call(functools.partial(kernel, n_e, n_s), out_shape=(pltpu.VMEM...]
where the time goes in v2:
time: 23.1 us; the launch traced here: 22.9 us
  Pallas kernels  22.3 us (97%)
  between operations  0.64 us (3%)
    pallas_call x1, Pallas kernels, local(): pl.pallas_call(functools.partial(kernel, n_e, n_s), out_shape=(pltpu.VMEM...  21 us
    pallas_call x1, Pallas kernels, local(): pl.pallas_call(finish, out_shape=(jax.ShapeDtypeStruct((rows, width), BF1...  1.22 us

profile of v2, /device:TPU:0, one launch (start us, length us, event | category | flops | bytes accessed | tf_op | source)
XLA Modules:
  0.0 22.9 jit_solution(10899674521348551400)
XLA Ops:
  0.6 21.0 %shard_map.131 = (bf16[128,1024]{1,0:T(8,128)(2,1)S(1)}, bf16[4,32,512]{2,1,0:T(8,128)(2,1)S(1)}, f32[4,32,128]{2,1,0:T(8,128)S(1)}, bf16[512,1024]{1,0:T(8,128)(2,1)S(1)}) custom-call(bf16[128,1024]{1,0:T(8,128)(2,1)} %tokens_h.1, s32[1,4,16]{2,1,0:T(4,128)} %picks_h.1, f32[1,4,16]{2,1,0:T(4,128)} %gates_h.1, s32[1,4]{1,0:T(1,128)} %counts_h.1, ...), custom_call_target="tpu_custom_call" | custom-call | tf_op jit(solution)/shard_map/pallas_call | solution.py:339
  21.7 1.2 %shard_map.132 = (bf16[128,1024]{1,0:T(8,128)(2,1)}, bf16[32,1024]{1,0:T(8,128)(2,1)}) custom-call(bf16[128,1024]{1,0:T(8,128)(2,1)S(1)} %get-tuple-element.6.enc_v, bf16[4,32,512]{2,1,0:T(8,128)(2,1)S(1)} %get-tuple-element.7.part_v, f32[4,32,128]{2,1,0:T(8,128)S(1)} %get-tuple-element.8.stat_v, bf16[512,1024]{1,0:T(8,128)(2,1)S(1)} %get-tuple-element.9.w_proj_v), custom_call_target="tpu_custom_call" | custom-call | tf_op jit(solution)/shard_map/pallas_call | solution.py:396

commit v3 on v2

--- a/solution.py
+++ b/solution.py
@@ -11,6 +11,8 @@
 EPSILON = 1e-06
 VMEM_BYTES = 67043328
 MESH = pl.DeviceIdType.MESH
+GATHER_PIECES = 1
+RETURN_PIECES = 1
 F32 = jnp.float32
 BF16 = jnp.bfloat16
 
@@ -41,7 +43,6 @@
     w_proj_h,
     enc_v,
     part_r,
-    stat_r,
     w_proj_v,
     tokens_v,
     picks_v,
@@ -59,7 +60,6 @@
     send_b,
     recv_b,
     part_v,
-    stat_v,
     load_sem,
     a_send,
     a_recv,
@@ -69,11 +69,10 @@
     q_recv,
     p_send,
     p_recv,
-    s_send,
-    s_recv,
 ):
     me_e = lax.axis_index("expert")
     me_s = lax.axis_index("seq")
+    upper = (2 * me_e) // n_e
     rows, width = tokens_v.shape
     slots = send_a.shape[1]
     dec_rows = q_v.shape[1]
@@ -117,25 +116,29 @@
     pick_row = jnp.concatenate([picks_v[0, j : j + 1, :] for j in range(n_e)], axis=1)
     position = lax.broadcasted_iota(jnp.int32, (rows, n_e * slots), 0)
     chosen = jnp.where(position == pick_row, 1.0, 0.0).astype(BF16)
-    outgoing = lax.dot_general(
-        chosen, normed, (((0,), (0,)), ((), ())), preferred_element_type=F32
-    ).astype(BF16)
-    send_a[...] = outgoing.reshape(n_e, slots, width)
-    pl.semaphore_wait(barrier, n_e - 1 + n_s - 1)
-
     a_copies = []
-    for d in range(1, n_e):
-        to = lax.rem(me_e + d, n_e)
-        copy = pltpu.make_async_remote_copy(
-            src_ref=send_a.at[to],
-            dst_ref=recv_a.at[d],
-            send_sem=a_send.at[d],
-            recv_sem=a_recv.at[d],
-            device_id={"expert": to},
-            device_id_type=MESH,
-        )
-        copy.start()
-        a_copies.append(copy)
+    piece = width // GATHER_PIECES
+    for c in range(GATHER_PIECES):
+        cols = slice(c * piece, (c + 1) * piece)
+        outgoing = lax.dot_general(
+            chosen, normed[:, cols], (((0,), (0,)), ((), ())), preferred_element_type=F32
+        ).astype(BF16)
+        send_a[:, :, cols] = outgoing.reshape(n_e, slots, piece)
+        if c == 0:
+            pl.semaphore_wait(barrier, n_e - 1 + n_s - 1)
+        for d in range(1, n_e):
+            off = d * upper + (n_e - d) * (1 - upper)
+            to = lax.rem(me_e + off, n_e)
+            copy = pltpu.make_async_remote_copy(
+                src_ref=send_a.at[to, :, cols],
+                dst_ref=recv_a.at[off, :, cols],
+                send_sem=a_send.at[c, off],
+                recv_sem=a_recv.at[c, off],
+                device_id={"expert": to},
+                device_id_type=MESH,
+            )
+            copy.start()
+            a_copies.append(copy)
     loads["queries"].wait()
     q_copies = []
     for d in range(1, n_s):
@@ -170,39 +173,54 @@
     combine = jnp.where(position_three == pick_three, gate_three, 0.0).astype(BF16)
 
     loads["w_in"].wait()
-    for copy in a_copies:
-        copy.wait_recv()
+    for c in range(GATHER_PIECES):
+        cols = slice(c * (width // GATHER_PIECES), (c + 1) * (width // GATHER_PIECES))
+        for d in range(1, n_e):
+            pltpu.make_async_remote_copy(
+                src_ref=send_a.at[lax.rem(me_e + d, n_e), :, cols],
+                dst_ref=recv_a.at[d, :, cols],
+                send_sem=a_send.at[c, d],
+                recv_sem=a_recv.at[c, d],
+                device_id={"expert": lax.rem(me_e + d, n_e)},
+                device_id_type=MESH,
+            ).wait_recv()
     flat = recv_a[...].reshape(n_e * slots, width)
     hidden = gelu(jnp.dot(flat, w_in_v[...], preferred_element_type=F32)).astype(BF16)
     loads["w_out"].wait()
-    result = jnp.dot(hidden, w_out_v[...], preferred_element_type=F32).astype(BF16)
-    send_b[...] = result.reshape(n_e, slots, width)
     b_copies = []
-    for d in range(1, n_e):
-        copy = pltpu.make_async_remote_copy(
-            src_ref=send_b.at[d],
-            dst_ref=recv_b.at[me_e],
-            send_sem=b_send.at[d],
-            recv_sem=b_recv.at[d],
-            device_id={"expert": lax.rem(me_e + n_e - d, n_e)},
-            device_id_type=MESH,
-        )
-        copy.start()
-        b_copies.append(copy)
+    piece = width // RETURN_PIECES
+    for c in range(RETURN_PIECES):
+        cols = slice(c * piece, (c + 1) * piece)
+        result = jnp.dot(hidden, w_out_v[:, cols], preferred_element_type=F32).astype(BF16)
+        send_b[:, :, cols] = result.reshape(n_e, slots, piece)
+        for d in range(1, n_e):
+            off = d * (1 - upper) + (n_e - d) * upper
+            copy = pltpu.make_async_remote_copy(
+                src_ref=send_b.at[off, :, cols],
+                dst_ref=recv_b.at[me_e, :, cols],
+                send_sem=b_send.at[c, off],
+                recv_sem=b_recv.at[c, off],
+                device_id={"expert": lax.rem(me_e + n_e - off, n_e)},
+                device_id_type=MESH,
+            )
+            copy.start()
+            b_copies.append(copy)
     recv_b[me_e] = send_b[0]
 
     loads["norm_out"].wait()
     loads["w_key"].wait()
     loads["w_value"].wait()
-    for d in range(1, n_e):
-        pltpu.make_async_remote_copy(
-            src_ref=send_b.at[d],
-            dst_ref=recv_b.at[lax.rem(me_e + d, n_e)],
-            send_sem=b_send.at[d],
-            recv_sem=b_recv.at[d],
-            device_id={"expert": lax.rem(me_e + n_e - d, n_e)},
-            device_id_type=MESH,
-        ).wait_recv()
+    for c in range(RETURN_PIECES):
+        cols = slice(c * piece, (c + 1) * piece)
+        for d in range(1, n_e):
+            pltpu.make_async_remote_copy(
+                src_ref=send_b.at[d, :, cols],
+                dst_ref=recv_b.at[lax.rem(me_e + d, n_e), :, cols],
+                send_sem=b_send.at[c, d],
+                recv_sem=b_recv.at[c, d],
+                device_id={"expert": lax.rem(me_e + n_e - d, n_e)},
+                device_id_type=MESH,
+            ).wait_recv()
     returned = recv_b[...].reshape(n_e * slots, width)
     expert_sum = jnp.dot(
         combine, jnp.concatenate([returned] * 3, axis=0), preferred_element_type=F32
@@ -227,9 +245,12 @@
     slab = min(256, q_width)
     group = slab // head
     lane_head = lax.broadcasted_iota(jnp.int32, (1, slab), 1) // head
-    stat_lane = lax.broadcasted_iota(jnp.int32, (1, stat_v.shape[2]), 1)
-    stats = jnp.zeros((all_rows, stat_v.shape[2]), F32)
-    for g in range(q_width // slab):
+    lanes = part_v.shape[2] - q_width
+    stat_lane = lax.broadcasted_iota(jnp.int32, (1, lanes), 1)
+    stats = jnp.zeros((all_rows, lanes), F32)
+    p_copies = []
+    groups = q_width // slab
+    for g in range(groups):
         cols = slice(g * slab, (g + 1) * slab)
         stacked = jnp.concatenate(
             [
@@ -254,27 +275,25 @@
             stats = jnp.where(stat_lane == at, row_max[span], stats)
             stats = jnp.where(stat_lane == HEADS + at, row_total[span], stats)
         part_v[:, :, cols] = joined.astype(BF16).reshape(n_s, dec_rows, slab)
-    stat_v[...] = stats.reshape(n_s, dec_rows, stat_v.shape[2])
-
-    part_r[0] = part_v[me_s]
-    stat_r[0] = stat_v[me_s]
-    p_copies = []
+        if g == groups - 1:
+            high = stats.astype(BF16).astype(F32)
+            middle = (stats - high).astype(BF16).astype(F32)
+            low = stats - high - middle
+            packed = high + pltpu.roll(middle, 2 * HEADS, 1) + pltpu.roll(low, 4 * HEADS, 1)
+            part_v[:, :, q_width:] = packed.astype(BF16).reshape(n_s, dec_rows, lanes)
     for d in range(1, n_s):
         to = lax.rem(me_s + d, n_s)
-        for src, dst, ss, rs in (
-            (stat_v, stat_r, s_send, s_recv),
-            (part_v, part_r, p_send, p_recv),
-        ):
-            copy = pltpu.make_async_remote_copy(
-                src_ref=src.at[to],
-                dst_ref=dst.at[d],
-                send_sem=ss.at[d],
-                recv_sem=rs.at[d],
-                device_id={"seq": to},
-                device_id_type=MESH,
-            )
-            copy.start()
-            p_copies.append(copy)
+        copy = pltpu.make_async_remote_copy(
+            src_ref=part_v.at[to],
+            dst_ref=part_r.at[d],
+            send_sem=p_send.at[d],
+            recv_sem=p_recv.at[d],
+            device_id={"seq": to},
+            device_id_type=MESH,
+        )
+        copy.start()
+        p_copies.append(copy)
+    part_r[0] = part_v[me_s]
     for copy in p_copies:
         copy.wait_recv()
     for copy in a_copies + b_copies + q_copies + p_copies:
@@ -283,14 +302,23 @@
 
 
 def finish(
-    enc_v, part_v, stat_v, w_proj_v, encoded_h, dec_h, dec_v, store_sem
+    enc_v, part_v, w_proj_v, encoded_h, dec_h, dec_v, store_sem
 ):
     enc_store = pltpu.make_async_copy(enc_v, encoded_h, store_sem.at[0])
     enc_store.start()
-    n_s, dec_rows, q_width = part_v.shape
+    n_s, dec_rows, _ = part_v.shape
+    q_width = w_proj_v.shape[0]
     head = q_width // HEADS
-    part = [part_v[d].astype(F32) for d in range(n_s)]
-    stat = [stat_v[d] for d in range(n_s)]
+    part = [part_v[d, :, :q_width].astype(F32) for d in range(n_s)]
+    stat = []
+    for d in range(n_s):
+        packed = part_v[d, :, q_width:].astype(F32)
+        lanes = packed.shape[1]
+        stat.append(
+            packed
+            + pltpu.roll(packed, lanes - 2 * HEADS, 1)
+            + pltpu.roll(packed, lanes - 4 * HEADS, 1)
+        )
     top = functools.reduce(jnp.maximum, stat)
     factor = [jnp.exp(s - top)[:, :HEADS] for s in stat]
     total = sum(f * s[:, HEADS : 2 * HEADS] for f, s in zip(factor, stat))
@@ -331,21 +359,20 @@
     slots = picks.shape[2]
     hidden = w_in.shape[2]
     dec_rows, q_width = queries.shape
-    lanes = max(128, 2 * HEADS)
+    lanes = 128 * pl.cdiv(6 * HEADS, 128)
     anywhere = pl.BlockSpec(memory_space=pl.ANY)
     dma = pltpu.SemaphoreType.DMA
     vmem = pl.BlockSpec(memory_space=pltpu.VMEM)
-    room = 2 * (rows * width + n_s * dec_rows * (q_width + 2 * lanes) + q_width * width)
-    encoded, part, stat, w_proj_near = pl.pallas_call(
+    room = 2 * (rows * width + n_s * dec_rows * (q_width + lanes) + q_width * width)
+    encoded, part, w_proj_near = pl.pallas_call(
         functools.partial(kernel, n_e, n_s),
         out_shape=(
             pltpu.VMEM((rows, width), BF16),
-            pltpu.VMEM((n_s, dec_rows, q_width), BF16),
-            pltpu.VMEM((n_s, dec_rows, lanes), F32),
+            pltpu.VMEM((n_s, dec_rows, q_width + lanes), BF16),
             pltpu.VMEM((q_width, width), BF16),
         ),
         in_specs=[anywhere] * 12,
-        out_specs=(vmem, vmem, vmem, vmem),
+        out_specs=(vmem, vmem, vmem),
         scratch_shapes=[
             pltpu.VMEM((rows, width), BF16),
             pltpu.VMEM(picks.shape, jnp.int32),
@@ -362,15 +389,12 @@
             pltpu.VMEM((n_e, slots, width), BF16),
             pltpu.VMEM((n_e, slots, width), BF16),
             pltpu.VMEM((n_e, slots, width), BF16),
-            pltpu.VMEM((n_s, dec_rows, q_width), BF16),
-            pltpu.VMEM((n_s, dec_rows, lanes), F32),
+            pltpu.VMEM((n_s, dec_rows, q_width + lanes), BF16),
             dma((12,)),
-            dma((n_e,)),
-            dma((n_e,)),
-            dma((n_e,)),
-            dma((n_e,)),
-            dma((n_s,)),
-            dma((n_s,)),
+            dma((GATHER_PIECES, n_e)),
+            dma((GATHER_PIECES, n_e)),
+            dma((RETURN_PIECES, n_e)),
+            dma((RETURN_PIECES, n_e)),
             dma((n_s,)),
             dma((n_s,)),
             dma((n_s,)),
@@ -399,11 +423,11 @@
             jax.ShapeDtypeStruct((rows, width), BF16),
             jax.ShapeDtypeStruct((dec_rows, width), BF16),
         ),
-        in_specs=[vmem] * 4,
+        in_specs=[vmem] * 3,
         out_specs=(anywhere, anywhere),
         scratch_shapes=[pltpu.VMEM((dec_rows, width), BF16), dma((2,))],
         compiler_params=pltpu.CompilerParams(vmem_limit_bytes=8 * 2**20),
-    )(encoded, part, stat, w_proj_near)
+    )(encoded, part, w_proj_near)
 
 
 def solution(mesh):

time: 23.1 us -> 21.5 us (0.931)
  Pallas kernels: 22.3 us -> 20.7 us
    pallas_call x1, Pallas kernels: 21 us -> 19.4 us  [local(): pl.pallas_call(functools.partial(kernel, n_e, n_s), out_shape=(pltpu.VMEM...]
where the time goes in v3:
time: 21.5 us; the launch traced here: 21.4 us
  Pallas kernels  20.7 us (96%)
  between operations  0.64 us (3%)
    pallas_call x1, Pallas kernels, local(): pl.pallas_call(functools.partial(kernel, n_e, n_s), out_shape=(pltpu.VMEM...  19.4 us
    pallas_call x1, Pallas kernels, local(): pl.pallas_call(finish, out_shape=(jax.ShapeDtypeStruct((rows, width), BF1...  1.3 us

profile of v3, /device:TPU:0, one launch (start us, length us, event | category | flops | bytes accessed | tf_op | source)
XLA Modules:
  0.0 21.4 jit_solution(17625423379707460386)
XLA Ops:
  0.6 19.4 %shard_map.131 = (bf16[128,1024]{1,0:T(8,128)(2,1)S(1)}, bf16[4,32,640]{2,1,0:T(8,128)(2,1)S(1)}, bf16[512,1024]{1,0:T(8,128)(2,1)S(1)}) custom-call(bf16[128,1024]{1,0:T(8,128)(2,1)} %tokens_h.1, s32[1,4,16]{2,1,0:T(4,128)} %picks_h.1, f32[1,4,16]{2,1,0:T(4,128)} %gates_h.1, s32[1,4]{1,0:T(1,128)} %counts_h.1, f32[1,1024]{1,0:T(1,128)} %bitcast.2, ...), custom_call_target="tpu_custom_call" | custom-call | tf_op jit(solution)/shard_map/pallas_call | solution.py:367
  20.1 1.3 %shard_map.132 = (bf16[128,1024]{1,0:T(8,128)(2,1)}, bf16[32,1024]{1,0:T(8,128)(2,1)}) custom-call(bf16[128,1024]{1,0:T(8,128)(2,1)S(1)} %get-tuple-element.5.enc_v, bf16[4,32,640]{2,1,0:T(8,128)(2,1)S(1)} %get-tuple-element.6.part_v, bf16[512,1024]{1,0:T(8,128)(2,1)S(1)} %get-tuple-element.7.w_proj_v), custom_call_target="tpu_custom_call" | custom-call | tf_op jit(solution)/shard_map/pallas_call | solution.py:420

commit v4 on v3

--- a/solution.py
+++ b/solution.py
@@ -79,6 +79,16 @@
     q_width = q_v.shape[2]
     head = q_width // HEADS
 
+    barrier = pltpu.get_barrier_semaphore()
+    for d in range(1, n_e):
+        pl.semaphore_signal(
+            barrier, inc=1, device_id={"expert": lax.rem(me_e + d, n_e)}, device_id_type=MESH
+        )
+    for d in range(1, n_s):
+        pl.semaphore_signal(
+            barrier, inc=1, device_id={"seq": lax.rem(me_s + d, n_s)}, device_id_type=MESH
+        )
+
     loads = {}
     for i, (name, src, dst) in enumerate(
         (
@@ -98,16 +108,6 @@
     ):
         loads[name] = pltpu.make_async_copy(src, dst, load_sem.at[i])
         loads[name].start()
-
-    barrier = pltpu.get_barrier_semaphore()
-    for d in range(1, n_e):
-        pl.semaphore_signal(
-            barrier, inc=1, device_id={"expert": lax.rem(me_e + d, n_e)}, device_id_type=MESH
-        )
-    for d in range(1, n_s):
-        pl.semaphore_signal(
-            barrier, inc=1, device_id={"seq": lax.rem(me_s + d, n_s)}, device_id_type=MESH
-        )
 
     loads["tokens"].wait()
     loads["norm_in"].wait()

time: 21.5 us -> 21.5 us (level)
  no operation moved by 1% of the time
where the time goes in v4:
time: 21.5 us; the launch traced here: 21.4 us
  Pallas kernels  20.7 us (96%)
  between operations  0.64 us (3%)
    pallas_call x1, Pallas kernels, local(): pl.pallas_call(functools.partial(kernel, n_e, n_s), out_shape=(pltpu.VMEM...  19.4 us
    pallas_call x1, Pallas kernels, local(): pl.pallas_call(finish, out_shape=(jax.ShapeDtypeStruct((rows, width), BF1...  1.3 us

profile of v4, /device:TPU:0, one launch (start us, length us, event | category | flops | bytes accessed | tf_op | source)
XLA Modules:
  0.0 21.4 jit_solution(3138432610193475253)
XLA Ops:
  0.6 19.4 %shard_map.131 = (bf16[128,1024]{1,0:T(8,128)(2,1)S(1)}, bf16[4,32,640]{2,1,0:T(8,128)(2,1)S(1)}, bf16[512,1024]{1,0:T(8,128)(2,1)S(1)}) custom-call(bf16[128,1024]{1,0:T(8,128)(2,1)} %tokens_h.1, s32[1,4,16]{2,1,0:T(4,128)} %picks_h.1, f32[1,4,16]{2,1,0:T(4,128)} %gates_h.1, s32[1,4]{1,0:T(1,128)} %counts_h.1, f32[1,1024]{1,0:T(1,128)} %bitcast.2, ...), custom_call_target="tpu_custom_call" | custom-call | tf_op jit(solution)/shard_map/pallas_call | solution.py:367
  20.1 1.3 %shard_map.132 = (bf16[128,1024]{1,0:T(8,128)(2,1)}, bf16[32,1024]{1,0:T(8,128)(2,1)}) custom-call(bf16[128,1024]{1,0:T(8,128)(2,1)S(1)} %get-tuple-element.5.enc_v, bf16[4,32,640]{2,1,0:T(8,128)(2,1)S(1)} %get-tuple-element.6.part_v, bf16[512,1024]{1,0:T(8,128)(2,1)S(1)} %get-tuple-element.7.w_proj_v), custom_call_target="tpu_custom_call" | custom-call | tf_op jit(solution)/shard_map/pallas_call | solution.py:420
